TPU v7x, 32 devices: a whole 2x2x4 slice. The times are simulated.
32 devices in a mesh: dp: 2 (over x), vocab: 16 (over z, y, core).
Axes of the slice: x: 2, y: 2, z: 4, core: 2. Of those that a mesh axis runs over, the one named last changes fastest.
Arguments:
- hidden: bfloat16 [96, 8192], P('dp', 'vocab'), may hold values from -90 to 90
- weight: bfloat16 [8192, 38016], P('dp', 'vocab'), may hold values from -0.1875 to 0.1875
- targets: int32 [96], P('dp'), may hold values from 0 to 38015
- pad_mask: int32 [96], P('dp'), may hold values from 0 to 1
Outputs:
- token_nll: float32 [96], P('dp')
- nll_total: float32 [], replicated
All inputs are finite; a program needn't handle non-finite values.
Results may differ from a plain program's by a relative error of at most 0.0003.
Values may be sent and summed in bfloat16 or wider, within the bound.
A program may use at most 64 MiB of HBM per device.

v0:
```python
import jax
import jax.numpy as jnp
from jax import lax
from jax.sharding import PartitionSpec as P


def merged_2(value, axis, join):
    pieces = jax.tree.map(lambda part: lax.all_gather(part, axis), value)
    head = jax.tree.map(lambda part: part[0], pieces)
    tail = jax.tree.map(lambda part: part[1:], pieces)
    subtotal, _ = lax.scan(lambda subtotal, share: (join(subtotal, share), None), head, tail)
    return subtotal


def join_stats(earlier, later):
    max_one, sum_one, pick_one = earlier
    max_two, sum_two, pick_two = later
    merged = jnp.maximum(max_one, max_two)
    return (
        merged,
        sum_one * jnp.exp(max_one - merged) + sum_two * jnp.exp(max_two - merged),
        pick_one + pick_two,
    )


def per_device(hidden, weight, targets, pad_mask):
    dp_size = lax.axis_size("dp")
    whole_width = lax.all_gather(hidden, "vocab", axis=1, tiled=True)
    tok_dev = whole_width.shape[0]
    n_cols = weight.shape[1]
    spread = lax.all_to_all(whole_width, "dp", split_axis=1, concat_axis=0, tiled=True)
    cols_sub = n_cols // dp_size
    logits = lax.psum_scatter(
        lax.dot_general(
            weight, spread, (((0,), (1,)), ((), ())), preferred_element_type=jnp.float32
        ),
        "dp",
        scatter_dimension=0,
        tiled=True,
    )
    all_targets, all_mask = (
        lax.all_gather(targets, "dp", axis=0, tiled=True),
        lax.all_gather(pad_mask, "dp", axis=0, tiled=True),
    )
    col_base = lax.axis_index("vocab") * n_cols + lax.axis_index("dp") * cols_sub
    column_ids = lax.broadcasted_iota(jnp.int32, (cols_sub, 1), 0) + col_base
    is_target = column_ids == all_targets[None, :]
    local_pick = jnp.sum(jnp.where(is_target, logits, 0.0), axis=0)
    local_max = jnp.max(logits, axis=0)
    local_sum = jnp.sum(jnp.exp(logits - local_max[None, :]), axis=0)
    row_max, exp_sum, picked = merged_2(
        (local_max, local_sum, local_pick), ("dp", "vocab"), join_stats
    )
    every_nll = all_mask.astype(jnp.float32) * (row_max + jnp.log(exp_sum) - picked)
    nll_total = jnp.sum(every_nll)
    token_nll = lax.dynamic_slice_in_dim(every_nll, lax.axis_index("dp") * tok_dev, tok_dev, 0)
    return (token_nll, nll_total)


def solution(mesh):
    placed = (P("dp", "vocab"), P("dp", "vocab"), P("dp"), P("dp"))
    return jax.shard_map(
        per_device, mesh=mesh, in_specs=placed, out_specs=(P("dp"), P()), check_vma=False
    )
```

profile of v0, /device:TPU:0, one launch (start us, length us, event | category | flops | bytes accessed | tf_op | source)
XLA Modules:
  0.0 145.3 jit_solution(8605927002165873996)
XLA Ops:
  7.2 0.0 copy-start
  7.2 0.0 copy-start.1
  7.2 0.0 copy-start.2
  7.2 0.0 all-reduce.10.cloned.1.call-start
  7.2 25.7 %all_gather.28 = bf16[48,8192]{1,0:T(8,128)(2,1)S(1)} all-gather(bf16[48,512]{1,0:T(8,128)(2,1)} %param.6), channel_id=1, replica_groups=mesh['dp'=2,'vocab'=16] {'vocab'}, dimensions={1}, use_global_device_ids=true | all-gather | bytes 835584 | tf_op jit(solution)/shard_map/all_gather | solution.py:28
  33.0 0.1 copy.12
  33.0 14.0 %all_to_all.19 = bf16[48,2,4096]{2,0,1:T(8,128)(2,1)S(1)} all-to-all(bf16[48,2,4096]{2,0,1:T(8,128)(2,1)S(1)} %bitcast.33), channel_id=1, replica_groups=mesh['dp'=2,'vocab'=16] {'dp'}, dimensions={1} | all-to-all | bytes 1572864 | tf_op jit(solution)/shard_map/all_to_all | solution.py:31
  47.0 11.1 %fusion.10 = f32[2376,96]{0,1:T(8,128)} fusion(bf16[4096,2376]{0,1:T(8,128)(2,1)} %param.7, bf16[96,4096]{1,0:T(8,128)(2,1)S(1)} %bitcast.32), kind=kOutput, calls=%fused_computation.18 | convolution fusion | flops 1868562432 | bytes 21163008 | tf_op jit(solution)/shard_map/dot_general | solution.py:34
  58.2 0.0 all-reduce.10.cloned.1.call-update
  58.2 0.0 copy-done
  58.2 0.7 fusion.9
  59.6 0.0 copy-done.1
  59.6 0.2 dynamic-update-slice
  59.8 0.0 copy-done.2
  59.8 0.2 dynamic-update-slice.3
  60.7 4.5 %all-reduce.6 = (s32[96]{0:T(128)S(1)}, s32[96]{0:T(128)S(1)}) all-reduce(s32[96]{0:T(128)S(1)} %dynamic-update-slice.3, s32[96]{0:T(128)S(1)} %dynamic-update-slice), channel_id=1, replica_groups=mesh['dp'=2,'vocab'=16] {'dp'}, use_global_device_ids=true, to_apply=%add.3 | all-reduce | flops 192 | bytes 1536
  65.2 26.8 %all-reduce.10.cloned.1.call-done = f32[2376,96]{0,1:T(8,128)} async-done(((f32[2376,96]{0,1:T(8,128)}), f32[2376,96]{0,1:T(8,128)}) %all-reduce.10.cloned.1.call-update) | async-done | bytes 912400
  92.0 1.3 dynamic-slice_reduce_fusion
  93.4 0.3 dynamic-update-slice.1
  93.7 1.4 select_reduce_fusion
  95.1 0.3 dynamic-update-slice.4
  95.3 0.3 dynamic-update-slice.2
  95.6 39.9 %all-reduce.7 = (f32[3072]{0:T(1024)S(1)}, f32[3072]{0:T(1024)S(1)}, f32[3072]{0:T(1024)S(1)}) all-reduce(f32[3072]{0:T(1024)S(1)} %dynamic-update-slice.1, f32[3072]{0:T(1024)S(1)} %dynamic-update-slice.2, f32[3072]{0:T(1024)S(1)} %dynamic-update-slice.4), channel_id=2, replica_groups=mesh['dp'=2,'vocab'=16] {'dp','vocab'}, use_global_device_ids=true, to_apply=%add.1 | all-reduce | flops 9216 | bytes 73728
  135.5 0.1 slice.33
  135.6 0.1 slice.34
  135.6 0.1 slice.35
  135.7 0.1 reshape.23
  135.8 0.1 reshape.24
  135.9 0.1 reshape.25
  135.9 1.4 while.14
  137.3 0.6 fusion.8
  137.9 0.6 dynamic_slice.13
  (40 shorter events, 1.0 us)
Async XLA Ops:
  7.2 51.1 %copy-start = (u32[32]{0:T(128)S(1)}, u32[32]{0:T(128)}, u32[]{:S(2)}) copy-start(u32[32]{0:T(128)} %constant.35) | copy-start | bytes 388
  7.2 52.4 %copy-start.1 = (s32[48]{0:T(128)S(1)}, s32[48]{0:T(128)}, u32[]{:S(2)}) copy-start(s32[48]{0:T(128)} %param.9) | copy-start | bytes 580
  7.2 52.6 %copy-start.2 = (s32[48]{0:T(128)S(1)}, s32[48]{0:T(128)}, u32[]{:S(2)}) copy-start(s32[48]{0:T(128)} %param.8) | copy-start | bytes 580
  7.2 84.8 %all-reduce.10.cloned.1.call-start = ((), (), s32[]{:S(2)}) async-start(), calls=%async_computation.1 | async-start | bytes 1867776
Sparse Core Ops, SparseCore 0:
  58.3 33.6 all-reduce.9
where the time goes:
time: 146 us; the launch traced here: 145 us
  blocking collectives  84.1 us (58%)
  waiting for transfers between devices  26.8 us (18%)
  between operations  15.5 us (11%)
  matrix products  11.1 us (8%)
  other arithmetic  4.28 us (3%)
  local copies, waits for them, and re-layouts  3.04 us (2%)
    unnamed x2, blocking collectives  44.4 us
    unnamed x2, waiting for transfers between devices  26.8 us
    all_gather x1, blocking collectives, per_device(): whole_width = lax.all_gather(hidden, 'vocab', axis=1, tiled=True)  25.7 us
    all_to_all x1, blocking collectives, per_device(): lax.all_to_all(whole_width, 'dp', split_axis=1, concat_axis=0, tiled=True)  14 us
    dot_general x1, matrix products, per_device(): lax.dot_general(weight, spread, (((0,), (1,)), ((), ())), preferred_eleme...  11.1 us
  transfers between devices with their start and end apart: 1, of which 1 were waited for; matrix products, arithmetic and copies ran while one was open for 1% of the time, Pallas kernels for 0%

commit v1 on v0

v1 whole, which is shorter than its diff:
```python
import functools

import jax
import jax.numpy as jnp
from jax import lax
from jax.experimental import pallas as pl
from jax.experimental.pallas import tpu as pltpu
from jax.sharding import PartitionSpec as P

N_CHUNKS = 3
LANES = 128
MESH = pl.DeviceIdType.MESH


def chunk_bounds(cols):
    width = max(LANES, cols // N_CHUNKS // LANES * LANES)
    starts = [i * width for i in range(N_CHUNKS)]
    return [(s, (cols - s) if i == N_CHUNKS - 1 else width) for i, s in enumerate(starts)]


def padded(width):
    return -(-width // LANES) * LANES


def kernel(n_dp, n_v, n_r, n_c, hid, w_hbm, tgt, msk, nll_out, tot_out,
           toks, w, acc, stat_in, stat_out, square,
           own_sem, w_sem, recv, line_send, plane_send, part_send,
           rs_send, rs_recv, st_send, st_recv, *codes):
    send_q, recv_q = codes[:N_CHUNKS], codes[N_CHUNKS:]
    t_loc, depth = hid.shape
    cols = w_hbm.shape[1]
    group = n_v // n_dp
    r_group = n_r // n_dp
    half = group // 2
    d = lax.axis_index("dp")
    v = lax.axis_index("vocab")
    k = lax.rem(v, 2)
    c = lax.rem(v // 2, n_c)
    r = v // (2 * n_c)

    def vid(rr, cc, kk):
        return (rr * n_c + cc) * 2 + kk

    def chunk_vid(i):
        k_off, idx = i // half, lax.rem(i, half)
        rr = d * r_group + lax.rem(idx // n_c + r, r_group)
        cc = lax.rem(idx + c, n_c)
        return vid(rr, cc, lax.rem(k + k_off, 2))

    def weight_copy(i):
        rows = pl.ds(pl.multiple_of((chunk_vid(i) - d * group) * depth, depth), depth)
        return pltpu.make_async_copy(w_hbm.at[rows, :], w.at[rows, :], w_sem.at[i])

    own = pltpu.make_async_copy(hid, toks.at[v, d], own_sem)
    own.start()

    def start_weight(i, carry):
        weight_copy(i).start()
        return carry

    lax.fori_loop(0, group, start_weight, 0)

    barrier = pltpu.get_barrier_semaphore()

    def greet(dd, vv):
        pl.semaphore_signal(barrier, inc=1, device_id={"dp": dd, "vocab": vv}, device_id_type=MESH)

    for o in range(1, n_r):
        greet(d, vid(lax.rem(r + o, n_r), c, k))
    for do in range(n_dp):
        for co in range(n_c):
            if do or co:
                greet(lax.rem(d + do, n_dp), vid(r, lax.rem(c + co, n_c), k))
    greet(d, vid(r, c, 1 - k))
    pl.semaphore_wait(barrier, n_r - 1 + n_dp * n_c - 1 + 1)

    def piece_copy(src, vv, dd, send_sem, to_d, to_v):
        return pltpu.make_async_remote_copy(
            src_ref=src, dst_ref=toks.at[vv, dd], send_sem=send_sem, recv_sem=recv.at[vv, dd],
            device_id={"dp": to_d, "vocab": to_v}, device_id_type=MESH)

    def arrived(vv, dd):
        pltpu.make_async_copy(hid, toks.at[vv, dd], recv.at[vv, dd]).wait()

    partner = vid(r, c, 1 - k)

    def line_copy(o):
        return piece_copy(hid, v, d, line_send.at[o], d, vid(lax.rem(r + o, n_r), c, k))

    def plane_copy(o, co):
        rr = lax.rem(r + o, n_r)
        mine = vid(rr, c, k)
        src = hid if o == 0 else toks.at[mine, d]
        return piece_copy(src, mine, d, plane_send.at[o, co], rr // r_group,
                          vid(r, lax.rem(c + co, n_c), k))

    def own_line_part(o):
        rr = lax.rem(r + o, n_r)
        mine = vid(rr, c, k)
        src = hid if o == 0 else toks.at[mine, d]
        return piece_copy(src, mine, d, part_send.at[mine // 2, d], d, partner)

    def spread(o, act):
        rr = lax.rem(r + o, n_r)
        home = rr // r_group == d
        for co in range(1, n_c):
            act(plane_copy(o, co))

        @pl.when(jnp.logical_not(home))
        def _():
            act(plane_copy(o, 0))

        @pl.when(home)
        def _():
            act(own_line_part(o))

    start = lambda copy: copy.start()
    sent = lambda copy: copy.wait_send()

    for o in range(1, n_r):
        line_copy(o).start()
    spread(0, start)
    for o in range(1, n_r):
        arrived(vid(lax.rem(r + o, n_r), c, k), d)
        spread(o, start)

    def plane_pieces(act):
        for ro in range(r_group):
            rr = d * r_group + lax.rem(r + ro, r_group)
            for do in range(n_dp):
                for co in range(n_c):
                    if do or co:
                        act(vid(rr, lax.rem(c + co, n_c), k), lax.rem(d + do, n_dp))

    def part_copy(vv, dd):
        return piece_copy(toks.at[vv, dd], vv, dd, part_send.at[vv // 2, dd], d, partner)

    def relay(vv, dd):
        arrived(vv, dd)
        part_copy(vv, dd).start()

    plane_pieces(relay)
    own.wait()

    def tokens_of(vv):
        return toks[vv].reshape(n_dp * t_loc, depth)

    def rows_of(vv):
        return pl.ds(pl.multiple_of((vv - d * group) * depth, depth), depth)

    def first_half(i, carry):
        vv = chunk_vid(i)
        weight_copy(i).wait()
        part = jnp.dot(tokens_of(vv), w[rows_of(vv), :], preferred_element_type=jnp.float32)
        part = part.reshape(n_dp, t_loc, cols)

        @pl.when(i == 0)
        def _():
            acc[...] = part

        @pl.when(i > 0)
        def _():
            acc[...] += part

        return carry

    lax.fori_loop(0, half, first_half, 0)

    def second_ready(i, carry):
        vv = chunk_vid(i)
        weight_copy(i).wait()
        for dd in range(n_dp):
            arrived(vv, dd)
        return carry

    lax.fori_loop(half, group, second_ready, 0)

    bounds = chunk_bounds(cols)

    def rs_copy(ch, o):
        peer = lax.rem(d + o, n_dp)
        return pltpu.make_async_remote_copy(
            src_ref=send_q[ch].at[peer], dst_ref=recv_q[ch].at[d],
            send_sem=rs_send.at[ch, o], recv_sem=rs_recv.at[ch, n_dp - o],
            device_id={"dp": peer}, device_id_type=MESH)

    for ch, (lo, width) in enumerate(bounds):
        cut = slice(lo, lo + width)
        total = acc[:, :, cut].reshape(n_dp * t_loc, width)
        for i in range(half, group):
            vv = chunk_vid(i)
            total += jnp.dot(tokens_of(vv), w[rows_of(vv), cut], preferred_element_type=jnp.float32)
        acc[:, :, cut] = total.reshape(n_dp, t_loc, width)
        for o in range(1, n_dp):
            peer = lax.rem(d + o, n_dp)
            mine = acc[peer, :, cut]
            top = jnp.maximum(jnp.max(jnp.abs(mine), axis=1, keepdims=True), 1e-30)
            expo = jnp.floor(jnp.log2(top)).astype(jnp.int32) + 2
            unit = jnp.exp2((15 - expo).astype(jnp.float32))
            code = jnp.round(mine * unit).astype(jnp.int32)
            send_q[ch][peer, :, :width] = code.astype(jnp.int16)
            wide = jnp.broadcast_to(expo, (t_loc, LANES))
            send_q[ch][peer, :, padded(width):] = wide.astype(jnp.int16)
            rs_copy(ch, o).start()

    maxes, sums, picks = [], [], []
    for ch, (lo, width) in enumerate(bounds):
        cut = slice(lo, lo + width)
        logits = acc[d, :, cut]
        for o in range(1, n_dp):
            src = lax.rem(d + n_dp - o, n_dp)
            pltpu.make_async_copy(send_q[ch].at[d], recv_q[ch].at[src], rs_recv.at[ch, n_dp - o]).wait()
            code = recv_q[ch][src, :, :width].astype(jnp.int32).astype(jnp.float32)
            expo = recv_q[ch][src, :, padded(width):].astype(jnp.int32)[:, :1]
            logits = logits + code * jnp.exp2((expo - 15).astype(jnp.float32))
        m = jnp.max(logits, axis=1, keepdims=True)
        ids = lax.broadcasted_iota(jnp.int32, (t_loc, width), 1) + (v * cols + lo)
        maxes.append(m)
        sums.append(jnp.sum(jnp.exp(logits - m), axis=1, keepdims=True))
        picks.append(jnp.sum(jnp.where(ids == tgt[...], logits, 0.0), axis=1, keepdims=True))
    top = functools.reduce(jnp.maximum, maxes)
    exp_sum = sum(s * jnp.exp(m - top) for s, m in zip(sums, maxes))
    pick = sum(picks)

    lane = lax.broadcasted_iota(jnp.int32, (t_loc, LANES), 1)
    mask = msk[...].astype(jnp.float32)
    packed = jnp.where(lane == 0, top, jnp.where(lane == 1, exp_sum, jnp.where(
        lane == 2, pick, jnp.where(lane == 3, mask, 0.0))))
    square[...] = jnp.zeros_like(square)
    square[:t_loc, :] = packed
    stat_out[...] = square[...].T[:8, :]
    stat_in[d, v] = stat_out[...]

    n_all = n_dp * n_v
    me = d * n_v + v

    def stat_copy(o):
        to = lax.rem(me + o, n_all)
        return pltpu.make_async_remote_copy(
            src_ref=stat_out, dst_ref=stat_in.at[d, v], send_sem=st_send.at[o],
            recv_sem=st_recv.at[n_all - o],
            device_id={"dp": to // n_v, "vocab": lax.rem(to, n_v)}, device_id_type=MESH)

    def start_stat(o, carry):
        stat_copy(o).start()
        return carry

    lax.fori_loop(1, n_all, start_stat, 0)

    def wait_stat(o, carry):
        src = lax.rem(me + o, n_all)
        pltpu.make_async_copy(
            stat_out, stat_in.at[src // n_v, lax.rem(src, n_v)], st_recv.at[o]).wait()
        return carry

    lax.fori_loop(1, n_all, wait_stat, 0)

    lane1 = lax.broadcasted_iota(jnp.int32, (1, LANES), 1)
    total = jnp.zeros((1, LANES), jnp.float32)
    for dd in range(n_dp):
        row = stat_in[dd]
        all_max = row[:, 0, :]
        m = jnp.max(all_max, axis=0, keepdims=True)
        s = jnp.sum(row[:, 1, :] * jnp.exp(all_max - m), axis=0, keepdims=True)
        p = jnp.sum(row[:, 2, :], axis=0, keepdims=True)
        nll = jnp.where(lane1 < t_loc, row[0, 3:4, :] * (m + jnp.log(s) - p), 0.0)
        total += nll

        @pl.when(d == dd)
        def _():
            nll_out[...] = nll[:, :t_loc]

    tot_out[...] = jnp.sum(total, axis=1, keepdims=True)

    for o in range(1, n_r):
        line_copy(o).wait_send()
    for o in range(n_r):
        spread(o, sent)
    plane_pieces(lambda vv, dd: part_copy(vv, dd).wait_send())
    for ch in range(N_CHUNKS):
        for o in range(1, n_dp):
            rs_copy(ch, o).wait_send()

    def end_stat(o, carry):
        stat_copy(o).wait_send()
        return carry

    lax.fori_loop(1, n_all, end_stat, 0)


def columns_of(n_chips):
    side = 1
    while side * side * 4 <= n_chips:
        side *= 2
    return side


def per_device(n_dp, n_v, hidden, weight, targets, pad_mask):
    t_loc, depth = hidden.shape
    rows, cols = weight.shape
    n_c = columns_of(n_v // 2)
    n_r = n_v // 2 // n_c
    widths = [padded(width) + LANES for _, width in chunk_bounds(cols)]
    dma = pltpu.SemaphoreType.DMA
    any_spec = pl.BlockSpec(memory_space=pl.ANY)
    vmem = pl.BlockSpec(memory_space=pltpu.VMEM)
    codes = [pltpu.VMEM((n_dp, t_loc, width), jnp.int16) for width in widths]
    nll, total = pl.pallas_call(
        functools.partial(kernel, n_dp, n_v, n_r, n_c),
        out_shape=(jax.ShapeDtypeStruct((1, t_loc), jnp.float32),
                   jax.ShapeDtypeStruct((1, 1), jnp.float32)),
        in_specs=[any_spec, any_spec, vmem, vmem],
        out_specs=(vmem, vmem),
        scratch_shapes=[
            pltpu.VMEM((n_v, n_dp, t_loc, depth), jnp.bfloat16),
            pltpu.VMEM((rows, cols), jnp.bfloat16),
            pltpu.VMEM((n_dp, t_loc, cols), jnp.float32),
            pltpu.VMEM((n_dp, n_v, 8, LANES), jnp.float32),
            pltpu.VMEM((8, LANES), jnp.float32),
            pltpu.VMEM((LANES, LANES), jnp.float32),
            dma, dma((n_v // n_dp,)), dma((n_v, n_dp)),
            dma((n_r,)), dma((n_r, n_c)), dma((n_v // 2, n_dp)),
            dma((N_CHUNKS, n_dp)), dma((N_CHUNKS, n_dp)),
            dma((n_dp * n_v,)), dma((n_dp * n_v,)),
            *codes, *codes,
        ],
        compiler_params=pltpu.CompilerParams(
            collective_id=0, has_side_effects=True, vmem_limit_bytes=60 * 1024 * 1024),
    )(hidden, weight, targets[:, None], pad_mask[:, None])
    return nll.reshape(t_loc), total.reshape(())


def solution(mesh):
    placed = (P("dp", "vocab"), P("dp", "vocab"), P("dp"), P("dp"))
    body = functools.partial(per_device, mesh.shape["dp"], mesh.shape["vocab"])
    return jax.shard_map(
        body, mesh=mesh, in_specs=placed, out_specs=(P("dp"), P()), check_vma=False
    )
```

time: 146 us -> 66.8 us (0.46)
  blocking collectives: 84.1 us -> 0 us
  Pallas kernels: 0 us -> 34.7 us
  waiting for transfers between devices: 26.8 us -> 0 us
  local copies, waits for them, and re-layouts: 3.04 us -> 29 us
  between operations: 15.5 us -> 2.34 us
  matrix products: 11.1 us -> 0 us
  other arithmetic: 4.28 us -> 0 us
    unnamed x2 -> x0, blocking collectives: 44.4 us -> none
    pallas_call x0 -> x1, Pallas kernels: none -> 34.7 us  [per_device(): pl.pallas_call(functools.partial(kernel, n_dp, n_v, n_r, n_c), out_shape=...]
    unnamed x2 -> x0, waiting for transfers between devices: 26.8 us -> none
    all_gather x1 -> x0, blocking collectives: 25.7 us -> none  [per_device(): whole_width = lax.all_gather(hidden, 'vocab', axis=1, tiled=True)]
    unnamed x17 -> x2, local copies, waits for them, and re-layouts: 1.97 us -> 26.3 us
    all_to_all x1 -> x0, blocking collectives: 14 us -> none  [per_device(): lax.all_to_all(whole_width, 'dp', split_axis=1, concat_axis=0, tiled=True)]
    dot_general x1 -> x0, matrix products: 11.1 us -> none  [per_device(): lax.dot_general(weight, spread, (((0,), (1,)), ((), ())), preferred_eleme...]
    broadcast_in_dim x0 -> x2, local copies, waits for them, and re-layouts: none -> 2.68 us  [the longest x1 1.34 us: per_device(): targets[:, None]]
  transfers between devices with their start and end apart: 1 -> 0, of which waited for: 1 -> 0; matrix products, arithmetic and copies ran while one was open for 1% -> 0% of each run, Pallas kernels for 0% -> 0%
where the time goes in v1:
time: 66.8 us; the launch traced here: 66 us
  Pallas kernels  34.7 us (52%)
  local copies, waits for them, and re-layouts  29 us (43%)
  between operations  2.34 us (4%)
    pallas_call x1, Pallas kernels, per_device(): pl.pallas_call(functools.partial(kernel, n_dp, n_v, n_r, n_c), out_shape=...  34.7 us
    unnamed x2, local copies, waits for them, and re-layouts  26.3 us
    broadcast_in_dim x1, local copies, waits for them, and re-layouts, per_device(): targets[:, None]  1.34 us
    broadcast_in_dim x1, local copies, waits for them, and re-layouts, per_device(): pad_mask[:, None]  1.34 us

profile of v1, /device:TPU:0, one launch (start us, length us, event | category | flops | bytes accessed | tf_op | source)
XLA Modules:
  0.0 66.0 jit_solution(18074753468419013143)
XLA Ops:
  0.6 1.3 %copy.7.tgt = s32[48,1]{1,0:T(8,128)} copy(s32[48,1]{0,1:T(1,128)} %bitcast.4) | data formatting | bytes 384 | tf_op jit(solution)/shard_map/broadcast_in_dim | solution.py:329
  2.0 1.3 %copy.8.msk = s32[48,1]{1,0:T(8,128)} copy(s32[48,1]{0,1:T(1,128)} %bitcast.5) | data formatting | bytes 384 | tf_op jit(solution)/shard_map/broadcast_in_dim | solution.py:329
  3.3 25.2 %copy.6.w_hbm = bf16[4096,2376]{1,0:T(8,128)(2,1)} copy(bf16[4096,2376]{0,1:T(8,128)(2,1)} %param.5) | data formatting | bytes 38928384 | tf_op args[1]
  28.5 34.7 %shard_map.59 = (f32[1,48]{1,0:T(1,128)}, f32[1,1]{1,0:T(1,128)}) custom-call(bf16[48,512]{1,0:T(8,128)(2,1)} %hid.1, bf16[4096,2376]{1,0:T(8,128)(2,1)} %copy.6.w_hbm, s32[48,1]{1,0:T(8,128)} %copy.7.tgt, s32[48,1]{1,0:T(8,128)} %copy.8.msk), custom_call_target="tpu_custom_call" | custom-call | tf_op jit(solution)/shard_map/pallas_call | solution.py:308
  63.2 1.1 %copy.11 = f32[48]{0:T(128)} copy(f32[48]{0:T(128)} %bitcast.6) | data formatting | bytes 384

commit v2 on v1

--- a/solution.py
+++ b/solution.py
@@ -22,13 +22,17 @@
     return -(-width // LANES) * LANES
 
 
+def product(tokens, heads):
+    return lax.dot_general(tokens, heads, (((1,), (1,)), ((), ())), preferred_element_type=jnp.float32)
+
+
 def kernel(n_dp, n_v, n_r, n_c, hid, w_hbm, tgt, msk, nll_out, tot_out,
            toks, w, acc, stat_in, stat_out, square,
            own_sem, w_sem, recv, line_send, plane_send, part_send,
            rs_send, rs_recv, st_send, st_recv, *codes):
     send_q, recv_q = codes[:N_CHUNKS], codes[N_CHUNKS:]
     t_loc, depth = hid.shape
-    cols = w_hbm.shape[1]
+    cols = w_hbm.shape[0]
     group = n_v // n_dp
     r_group = n_r // n_dp
     half = group // 2
@@ -49,7 +53,7 @@
 
     def weight_copy(i):
         rows = pl.ds(pl.multiple_of((chunk_vid(i) - d * group) * depth, depth), depth)
-        return pltpu.make_async_copy(w_hbm.at[rows, :], w.at[rows, :], w_sem.at[i])
+        return pltpu.make_async_copy(w_hbm.at[:, rows], w.at[:, rows], w_sem.at[i])
 
     own = pltpu.make_async_copy(hid, toks.at[v, d], own_sem)
     own.start()
@@ -151,7 +155,7 @@
     def first_half(i, carry):
         vv = chunk_vid(i)
         weight_copy(i).wait()
-        part = jnp.dot(tokens_of(vv), w[rows_of(vv), :], preferred_element_type=jnp.float32)
+        part = product(tokens_of(vv), w[:, rows_of(vv)])
         part = part.reshape(n_dp, t_loc, cols)
 
         @pl.when(i == 0)
@@ -189,7 +193,7 @@
         total = acc[:, :, cut].reshape(n_dp * t_loc, width)
         for i in range(half, group):
             vv = chunk_vid(i)
-            total += jnp.dot(tokens_of(vv), w[rows_of(vv), cut], preferred_element_type=jnp.float32)
+            total += product(tokens_of(vv), w[cut, rows_of(vv)])
         acc[:, :, cut] = total.reshape(n_dp, t_loc, width)
         for o in range(1, n_dp):
             peer = lax.rem(d + o, n_dp)
@@ -203,6 +207,9 @@
             send_q[ch][peer, :, padded(width):] = wide.astype(jnp.int16)
             rs_copy(ch, o).start()
 
+    square[...] = jnp.zeros_like(square)
+    square[:, :t_loc] = jnp.broadcast_to(tgt[...].astype(jnp.float32), (LANES, t_loc))
+    wanted = square[...].T[:t_loc, :1].astype(jnp.int32)
     maxes, sums, picks = [], [], []
     for ch, (lo, width) in enumerate(bounds):
         cut = slice(lo, lo + width)
@@ -217,18 +224,17 @@
         ids = lax.broadcasted_iota(jnp.int32, (t_loc, width), 1) + (v * cols + lo)
         maxes.append(m)
         sums.append(jnp.sum(jnp.exp(logits - m), axis=1, keepdims=True))
-        picks.append(jnp.sum(jnp.where(ids == tgt[...], logits, 0.0), axis=1, keepdims=True))
+        picks.append(jnp.sum(jnp.where(ids == wanted, logits, 0.0), axis=1, keepdims=True))
     top = functools.reduce(jnp.maximum, maxes)
     exp_sum = sum(s * jnp.exp(m - top) for s, m in zip(sums, maxes))
     pick = sum(picks)
 
     lane = lax.broadcasted_iota(jnp.int32, (t_loc, LANES), 1)
-    mask = msk[...].astype(jnp.float32)
-    packed = jnp.where(lane == 0, top, jnp.where(lane == 1, exp_sum, jnp.where(
-        lane == 2, pick, jnp.where(lane == 3, mask, 0.0))))
+    packed = jnp.where(lane == 0, top, jnp.where(lane == 1, exp_sum, jnp.where(lane == 2, pick, 0.0)))
     square[...] = jnp.zeros_like(square)
     square[:t_loc, :] = packed
     stat_out[...] = square[...].T[:8, :]
+    stat_out[3:4, :t_loc] = msk[...].astype(jnp.float32)
     stat_in[d, v] = stat_out[...]
 
     n_all = n_dp * n_v
@@ -313,7 +319,7 @@
         out_specs=(vmem, vmem),
         scratch_shapes=[
             pltpu.VMEM((n_v, n_dp, t_loc, depth), jnp.bfloat16),
-            pltpu.VMEM((rows, cols), jnp.bfloat16),
+            pltpu.VMEM((cols, rows), jnp.bfloat16),
             pltpu.VMEM((n_dp, t_loc, cols), jnp.float32),
             pltpu.VMEM((n_dp, n_v, 8, LANES), jnp.float32),
             pltpu.VMEM((8, LANES), jnp.float32),
@@ -326,7 +332,7 @@
         ],
         compiler_params=pltpu.CompilerParams(
             collective_id=0, has_side_effects=True, vmem_limit_bytes=60 * 1024 * 1024),
-    )(hidden, weight, targets[:, None], pad_mask[:, None])
+    )(hidden, weight.T, targets[None, :], pad_mask[None, :])
     return nll.reshape(t_loc), total.reshape(())
 
 

time: 66.8 us -> 41.1 us (0.62)
  local copies, waits for them, and re-layouts: 29 us -> 1.11 us
  Pallas kernels: 34.7 us -> 37.4 us
    unnamed x2 -> x1, local copies, waits for them, and re-layouts: 26.3 us -> 1.11 us
    pallas_call x1, Pallas kernels: 34.7 us -> 37.4 us  [per_device(): pl.pallas_call(functools.partial(kernel, n_dp, n_v, n_r, n_c), out_shape=...]
    broadcast_in_dim x2 -> x0, local copies, waits for them, and re-layouts: 2.68 us -> none  [the longest x1 1.34 us: per_device(): targets[:, None]]
where the time goes in v2:
time: 41.1 us; the launch traced here: 40.9 us
  Pallas kernels  37.4 us (91%)
  between operations  2.4 us (6%)
  local copies, waits for them, and re-layouts  1.11 us (3%)
    pallas_call x1, Pallas kernels, per_device(): pl.pallas_call(functools.partial(kernel, n_dp, n_v, n_r, n_c), out_shape=...  37.4 us
    unnamed x1, local copies, waits for them, and re-layouts  1.11 us

profile of v2, /device:TPU:0, one launch (start us, length us, event | category | flops | bytes accessed | tf_op | source)
XLA Modules:
  0.0 40.9 jit_solution(17291517184416211312)
XLA Ops:
  0.6 37.4 %shard_map.59 = (f32[1,48]{1,0:T(1,128)}, f32[1,1]{1,0:T(1,128)}) custom-call(bf16[48,512]{1,0:T(8,128)(2,1)} %hid.1, bf16[2376,4096]{1,0:T(8,128)(2,1)} %bitcast.5, s32[1,48]{1,0:T(1,128)} %bitcast.6, s32[1,48]{1,0:T(1,128)} %bitcast.7), custom_call_target="tpu_custom_call" | custom-call | tf_op jit(solution)/shard_map/pallas_call | solution.py:314
  38.0 1.1 %copy.8 = f32[48]{0:T(128)} copy(f32[48]{0:T(128)} %bitcast.8) | data formatting | bytes 384

commit v3 on v2

--- a/solution.py
+++ b/solution.py
@@ -7,7 +7,7 @@
 from jax.experimental.pallas import tpu as pltpu
 from jax.sharding import PartitionSpec as P
 
-N_CHUNKS = 3
+N_CHUNKS = 4
 LANES = 128
 MESH = pl.DeviceIdType.MESH
 
@@ -41,6 +41,7 @@
     k = lax.rem(v, 2)
     c = lax.rem(v // 2, n_c)
     r = v // (2 * n_c)
+    way = 2 * (r // max(1, n_r // 2)) - 1
 
     def vid(rr, cc, kk):
         return (rr * n_c + cc) * 2 + kk
@@ -89,23 +90,23 @@
     partner = vid(r, c, 1 - k)
 
     def line_copy(o):
-        return piece_copy(hid, v, d, line_send.at[o], d, vid(lax.rem(r + o, n_r), c, k))
+        return piece_copy(hid, v, d, line_send.at[o], d, vid(lax.rem(r + n_r + way * o, n_r), c, k))
 
     def plane_copy(o, co):
-        rr = lax.rem(r + o, n_r)
+        rr = lax.rem(r + n_r - way * o, n_r)
         mine = vid(rr, c, k)
         src = hid if o == 0 else toks.at[mine, d]
         return piece_copy(src, mine, d, plane_send.at[o, co], rr // r_group,
                           vid(r, lax.rem(c + co, n_c), k))
 
     def own_line_part(o):
-        rr = lax.rem(r + o, n_r)
+        rr = lax.rem(r + n_r - way * o, n_r)
         mine = vid(rr, c, k)
         src = hid if o == 0 else toks.at[mine, d]
         return piece_copy(src, mine, d, part_send.at[mine // 2, d], d, partner)
 
     def spread(o, act):
-        rr = lax.rem(r + o, n_r)
+        rr = lax.rem(r + n_r - way * o, n_r)
         home = rr // r_group == d
         for co in range(1, n_c):
             act(plane_copy(o, co))
@@ -125,7 +126,7 @@
         line_copy(o).start()
     spread(0, start)
     for o in range(1, n_r):
-        arrived(vid(lax.rem(r + o, n_r), c, k), d)
+        arrived(vid(lax.rem(r + n_r - way * o, n_r), c, k), d)
         spread(o, start)
 
     def plane_pieces(act):

time: 41.1 us -> 39.6 us (0.964)
  Pallas kernels: 37.4 us -> 35.9 us
    pallas_call x1, Pallas kernels: 37.4 us -> 35.9 us  [per_device(): pl.pallas_call(functools.partial(kernel, n_dp, n_v, n_r, n_c), out_shape=...]
where the time goes in v3:
time: 39.6 us; the launch traced here: 39.4 us
  Pallas kernels  35.9 us (91%)
  between operations  2.4 us (6%)
  local copies, waits for them, and re-layouts  1.11 us (3%)
    pallas_call x1, Pallas kernels, per_device(): pl.pallas_call(functools.partial(kernel, n_dp, n_v, n_r, n_c), out_shape=...  35.9 us
    unnamed x1, local copies, waits for them, and re-layouts  1.11 us

profile of v3, /device:TPU:0, one launch (start us, length us, event | category | flops | bytes accessed | tf_op | source)
XLA Modules:
  0.0 39.4 jit_solution(5792152240255535747)
XLA Ops:
  0.6 35.9 %shard_map.59 = (f32[1,48]{1,0:T(1,128)}, f32[1,1]{1,0:T(1,128)}) custom-call(bf16[48,512]{1,0:T(8,128)(2,1)} %hid.1, bf16[2376,4096]{1,0:T(8,128)(2,1)} %bitcast.5, s32[1,48]{1,0:T(1,128)} %bitcast.6, s32[1,48]{1,0:T(1,128)} %bitcast.7), custom_call_target="tpu_custom_call" | custom-call | tf_op jit(solution)/shard_map/pallas_call | solution.py:315
  36.6 1.1 %copy.8 = f32[48]{0:T(128)} copy(f32[48]{0:T(128)} %bitcast.8) | data formatting | bytes 384
